TPU v7x, 32 devices: a whole 2x2x4 slice. The times are simulated.
32 devices in a mesh: groups: 2 (over y), seq: 4 (over z), tensor: 4 (over x, core).
Axes of the slice: x: 2, y: 2, z: 4, core: 2. Of those that a mesh axis runs over, the one named last changes fastest.
Arguments:
- final_block_queries: bfloat16 [256, 8192], P(('groups', 'seq'), 'tensor'), parts along dimension 0, may hold values from -96 to 96
- final_block_keys: bfloat16 [256, 1024], P(('groups', 'seq'), 'tensor'), parts along dimension 0, may hold values from -16 to 16
- final_block_values: bfloat16 [256, 1024], P(('groups', 'seq'), 'tensor'), parts along dimension 0, may hold values from -6 to 6
- prompt_cached_keys: bfloat16 [12288, 1024], P(('groups', 'seq'), 'tensor'), parts along dimension 0, may hold values from -16 to 16
- prompt_cached_values: bfloat16 [12288, 1024], P(('groups', 'seq'), 'tensor'), parts along dimension 0, may hold values from -6 to 6
- paged_cache_pool: bfloat16 [256, 128, 2, 1024], P(('groups', 'seq'), None, None, 'tensor'), parts along dimension 0, may hold values from -16 to 16
- step_slot_queries: bfloat16 [32, 4, 8192], P(('groups', 'seq'), None, 'tensor'), parts along dimension 0, may hold values from -96 to 96
- step_token_keys: bfloat16 [32, 4, 1024], P(('groups', 'seq'), None, 'tensor'), parts along dimension 0, may hold values from -16 to 16
- step_token_values: bfloat16 [32, 4, 1024], P(('groups', 'seq'), None, 'tensor'), parts along dimension 0, may hold values from -6 to 6
- normed_step_inputs: bfloat16 [32, 4, 8192], P(('groups', 'seq'), None, 'tensor'), parts along dimension 0, may hold values from -6 to 6
- adapter_down_maps: bfloat16 [8192, 128], P('tensor'), may hold values from -0.0625 to 0.0625
- adapter_up_maps: bfloat16 [128, 8192], P(None, 'tensor'), may hold values from -1.5 to 1.5
- slot_request: int32 [32], P('groups'), parts along dimension 0, may hold values from 0 to 15, as said below
- request_page_table: int32 [32, 8], P('groups'), parts along dimension 0, may hold values from 0 to 127, as said below
- lengths: int32 [32], P('groups'), parts along dimension 0, may hold values from 2 to 1024, as said below
- request_adapter: int32 [32], P('groups'), parts along dimension 0, may hold values from 0 to 7
- request_rank: int32 [32], P('groups'), parts along dimension 0, may hold values from 4 to 16
Outputs:
- prefill_out: bfloat16 [256, 8192], P(('groups', 'seq'), 'tensor'), parts along dimension 0
- decode_out: bfloat16 [32, 4, 8192], P(('groups', 'seq'), None, 'tensor'), parts along dimension 0
There are 2 independent parts, one for each index of `groups`. A program takes and returns all parts, laid end to end along the dimension named above; an argument that names none is the same for every part. Nothing has to cross between parts.
Inputs may be any that keep to these rules, and one draw needn't show every extreme that they name: A permutation: slot k serves request slot_request[k]; the owner of slots k * 4 to (k + 1) * 4 - 1 is owner k. `request_page_table`: every pool page is named exactly once. For every owner and every block of 32 pool pages (pages b * 32 to (b + 1) * 32 - 1), exactly 8 of the pages of that owner's requests lie in the block. `lengths`: some request has exactly 1024 cached tokens.
All inputs are finite; a program needn't handle non-finite values.
Results may differ from a plain program's by a relative error of at most 0.028.
Values may be sent and summed in bfloat16 or wider, within the bound.
No kernel may reach another device: no remote copies, remote signals or barrier semaphores. Data moves between devices by JAX's collectives and lax.ppermute only.
A program may use at most 128 MiB of HBM per device.

v0:
```python
import jax
import jax.numpy as jnp
from jax import lax
from jax.sharding import PartitionSpec as P

HEAD_SIZE = 128
LARGEST_RANK = 16
MASKED = -1e30


def lookup_rows(lookup, positions):
    hit_mask = positions[..., None] == jnp.arange(lookup.shape[0], dtype=jnp.int32)
    if lookup.ndim == 1:
        return jnp.sum(jnp.where(hit_mask, lookup, 0), axis=-1)
    return jnp.sum(jnp.where(hit_mask[..., None], lookup, 0), axis=-2)


def partial_softmax(query_vectors, paged_key_rows, paged_value_rows, allowed):
    batch_count, query_total_count, query_width = query_vectors.shape
    kv_heads = paged_key_rows.shape[2] // HEAD_SIZE
    heads_per_group = query_width // HEAD_SIZE // kv_heads
    query_head_rows = query_vectors.reshape(
        batch_count, query_total_count, kv_heads, heads_per_group, HEAD_SIZE
    )
    key_head_rows = paged_key_rows.reshape(
        batch_count, paged_key_rows.shape[1], kv_heads, HEAD_SIZE
    )
    value_head_rows = paged_value_rows.reshape(
        batch_count, paged_value_rows.shape[1], kv_heads, HEAD_SIZE
    )
    scores = jnp.einsum(
        "etkgd,epkd->ekgtp", query_head_rows, key_head_rows, preferred_element_type=jnp.float32
    ) * HEAD_SIZE ** (-0.5)
    key_mask = allowed[:, None, None, :, :]
    scores = jnp.where(key_mask, scores, MASKED)
    row_max = jnp.max(scores, axis=-1)
    weights = jnp.where(key_mask, jnp.exp(scores - row_max[..., None]), 0.0)
    row_total = jnp.sum(weights, axis=-1)
    summed = jnp.einsum(
        "ekgtp,epkd->etkgd",
        weights.astype(jnp.bfloat16),
        value_head_rows,
        preferred_element_type=jnp.float32,
    )
    heads_here = kv_heads * heads_per_group
    row_max = jnp.transpose(row_max, (0, 3, 1, 2)).reshape(
        batch_count, query_total_count, heads_here
    )
    row_total = jnp.transpose(row_total, (0, 3, 1, 2)).reshape(
        batch_count, query_total_count, heads_here
    )
    return (
        summed.reshape(batch_count, query_total_count, heads_here, HEAD_SIZE),
        row_max,
        row_total,
    )


def combine(summed, row_max, row_total, along):
    best_max = jnp.max(row_max, axis=along, keepdims=True)
    factor = jnp.exp(row_max - best_max)
    whole_total = jnp.sum(factor * row_total, axis=along)
    merged = jnp.sum(factor[..., None] * summed, axis=along)
    return merged / whole_total[..., None]


def per_device(
    final_block_queries,
    final_block_keys,
    final_block_values,
    prompt_cached_keys,
    prompt_cached_values,
    paged_cache_pool,
    step_slot_queries,
    step_token_keys,
    step_token_values,
    normed_step_inputs,
    adapter_down_maps,
    adapter_up_maps,
    slot_request,
    request_page_table,
    lengths,
    request_adapter,
    request_rank,
):
    seq_count = lax.axis_size("seq")
    position = lax.axis_index("seq")
    span_rows = final_block_queries.shape[0]
    ctx_rows = prompt_cached_keys.shape[0]
    heads_here = final_block_queries.shape[1] // HEAD_SIZE
    everyone = lax.all_gather(final_block_queries, "seq", axis=0, tiled=True)
    span_total = everyone.shape[0]
    block_rows = min(128, span_total)
    paged_key_rows = jnp.concatenate([prompt_cached_keys, final_block_keys], axis=0)
    paged_value_rows = jnp.concatenate([prompt_cached_values, final_block_values], axis=0)
    spots = jnp.arange(paged_key_rows.shape[0], dtype=jnp.int32)
    key_pos = jnp.where(spots < ctx_rows, -1, position * span_rows + spots - ctx_rows)

    def run_block(row_start):
        query_rows = lax.dynamic_slice_in_dim(everyone, row_start, block_rows, 0)
        row_pos = row_start + jnp.arange(block_rows, dtype=jnp.int32)
        allowed = key_pos[None, :] <= row_pos[:, None]
        summed, row_max, row_total = partial_softmax(
            query_rows[None], paged_key_rows[None], paged_value_rows[None], allowed[None]
        )
        return (summed[0], row_max[0], row_total[0])

    starts = jnp.arange(span_total // block_rows, dtype=jnp.int32) * block_rows
    summed, row_max, row_total = lax.map(run_block, starts)
    summed = summed.reshape(span_total, heads_here, HEAD_SIZE)
    row_max = row_max.reshape(span_total, heads_here)
    row_total = row_total.reshape(span_total, heads_here)
    returned = (
        lax.all_to_all(summed, "seq", split_axis=0, concat_axis=0, tiled=True),
        lax.all_to_all(row_max, "seq", split_axis=0, concat_axis=0, tiled=True),
        lax.all_to_all(row_total, "seq", split_axis=0, concat_axis=0, tiled=True),
    )
    block_sums = returned[0].reshape(seq_count, span_rows, heads_here, HEAD_SIZE)
    block_maxes = returned[1].reshape(seq_count, span_rows, heads_here)
    block_totals = returned[2].reshape(seq_count, span_rows, heads_here)
    prefill_out = (
        combine(block_sums, block_maxes, block_totals, 0)
        .reshape(span_rows, heads_here * HEAD_SIZE)
        .astype(jnp.bfloat16)
    )
    slots_total = slot_request.shape[0]
    slots_here = slots_total // seq_count
    page_count = request_page_table.shape[1]
    pool_here = paged_cache_pool.shape[0]
    page_len = paged_cache_pool.shape[1]
    per_owner = slots_here * page_count // seq_count
    entries = slots_here * page_count
    decode_step_count = step_slot_queries.shape[1]
    slot_page_list = lookup_rows(request_page_table, slot_request)
    slot_length = lookup_rows(lengths, slot_request)
    owner_pages = slot_page_list.reshape(seq_count, entries)
    holder = owner_pages // pool_here
    pool_place = owner_pages % pool_here
    is_mine = holder == position
    rank_in = jnp.cumsum(is_mine.astype(jnp.int32), axis=1) - 1
    hit_mask = is_mine[:, :, None] & (rank_in[:, :, None] == jnp.arange(per_owner, dtype=jnp.int32))
    send_place = jnp.sum(jnp.where(hit_mask, pool_place[:, :, None], 0), axis=1).reshape(-1)
    entry_ids = jnp.arange(entries, dtype=jnp.int32)
    outgoing = paged_cache_pool[send_place]
    my_holder = lax.dynamic_index_in_dim(holder, position, 0, keepdims=False)
    before = (my_holder[None, :] == my_holder[:, None]) & (entry_ids[None, :] < entry_ids[:, None])
    arrive = my_holder * per_owner + jnp.sum(before.astype(jnp.int32), axis=1)
    my_requests = lax.dynamic_slice_in_dim(slot_request, position * slots_here, slots_here)
    my_lengths = lax.dynamic_slice_in_dim(slot_length, position * slots_here, slots_here)
    adapters = lookup_rows(request_adapter, my_requests)
    ranks = lookup_rows(request_rank, my_requests)
    hidden_input_rows = normed_step_inputs.reshape(
        slots_here * decode_step_count, normed_step_inputs.shape[2]
    )
    reduced_rank_state = lax.psum(
        jnp.dot(hidden_input_rows, adapter_down_maps, preferred_element_type=jnp.float32), "tensor"
    )
    column_indices = jnp.arange(adapter_down_maps.shape[1], dtype=jnp.int32)
    rank_keep_mask = (column_indices[None, :] // LARGEST_RANK == adapters[:, None]) & (
        column_indices[None, :] % LARGEST_RANK < ranks[:, None]
    )
    adapter_kept_rank = jnp.where(
        jnp.repeat(rank_keep_mask, decode_step_count, axis=0), reduced_rank_state, 0.0
    ).astype(jnp.bfloat16)
    raised_queries = jnp.dot(
        adapter_kept_rank, adapter_up_maps, preferred_element_type=jnp.float32
    ).reshape(slots_here, decode_step_count, -1)
    query_vectors = (step_slot_queries.astype(jnp.float32) + raised_queries).astype(jnp.bfloat16)
    step_pos = jnp.arange(decode_step_count, dtype=jnp.int32)
    fresh_ok = step_pos[None, :] <= step_pos[:, None]
    incoming = lax.all_to_all(outgoing, "seq", split_axis=0, concat_axis=0, tiled=True)
    gathered_pages = incoming[arrive].reshape(slots_here, page_count * page_len, 2, -1)
    all_keys = jnp.concatenate([gathered_pages[:, :, 0], step_token_keys], axis=1)
    all_values = jnp.concatenate([gathered_pages[:, :, 1], step_token_values], axis=1)
    cache_pos = jnp.arange(page_count * page_len, dtype=jnp.int32)
    cache_ok = jnp.broadcast_to(
        cache_pos[None, None, :] < my_lengths[:, None, None],
        (slots_here, decode_step_count, page_count * page_len),
    )
    allowed = jnp.concatenate(
        [
            cache_ok,
            jnp.broadcast_to(fresh_ok[None], (slots_here, decode_step_count, decode_step_count)),
        ],
        axis=2,
    )
    summed, row_max, row_total = partial_softmax(query_vectors, all_keys, all_values, allowed)
    decode_out = (
        (summed / row_total[..., None])
        .reshape(slots_here, decode_step_count, -1)
        .astype(jnp.bfloat16)
    )
    return (prefill_out, decode_out)


def solution(mesh):
    placed = (
        P(("groups", "seq"), "tensor"),
        P(("groups", "seq"), "tensor"),
        P(("groups", "seq"), "tensor"),
        P(("groups", "seq"), "tensor"),
        P(("groups", "seq"), "tensor"),
        P(("groups", "seq"), None, None, "tensor"),
        P(("groups", "seq"), None, "tensor"),
        P(("groups", "seq"), None, "tensor"),
        P(("groups", "seq"), None, "tensor"),
        P(("groups", "seq"), None, "tensor"),
        P("tensor", None),
        P(None, "tensor"),
        P("groups"),
        P("groups", None),
        P("groups"),
        P("groups"),
        P("groups"),
    )
    return jax.shard_map(
        per_device,
        mesh=mesh,
        in_specs=placed,
        out_specs=(P(("groups", "seq"), "tensor"), P(("groups", "seq"), None, "tensor")),
        check_vma=False,
    )
```

profile of v0, /device:TPU:0, one launch (start us, length us, event | category | flops | bytes accessed | tf_op | source)
XLA Modules:
  0.0 200.9 jit_solution(16508769630650685992)
XLA Ops:
  0.7 0.3 iota_compare_fusion
  0.9 1.2 pad_maximum_fusion
  2.2 0.7 copy.124
  2.8 17.6 %all_gather.3 = bf16[128,2048]{1,0:T(8,128)(2,1)S(1)} all-gather(bf16[32,2048]{1,0:T(8,128)(2,1)} %param.17), channel_id=1, replica_groups=mesh['groups'=2,'seq'=4,'tensor'=4] {'seq'}, dimensions={0}, use_global_device_ids=true | all-gather | bytes 655360 | tf_op jit(solution)/shard_map/all_gather | solution.py:91
  20.4 0.3 copy.125
  20.7 2.0 %fusion.1 = (f32[2,8,128]{2,1,0:T(8,128)S(1)}, f32[2,1568,128,8]{2,1,3,0:T(8,128)S(1)}) fusion(pred[128,1568]{0,1:T(8,128)(4,1)S(1)} %iota_compare_fusion, bf16[1568,2,128,1]{0,2,3,1:T(8,128)(2,1)S(1)} %bitcast.128, bf16[128,2,8,128]{0,3,2,1:T(8,128)(2,1)S(1)} %bitcast.129), kind=kOutput, calls=%fused_computation.5 | convolution fusion | flops 831715328 | bytes 14381056 | tf_op jit(solution)/shard_map/while/body/eval_jaxpr/etkgd,epkd->ekgtp/dot_general | solution.py:31
  22.8 3.0 %fusion.2 = f32[2,8,128]{2,1,0:T(8,128)S(1)} fusion(f32[2,1568,128,8]{2,1,3,0:T(8,128)S(1)} %get-tuple-element.36, f32[2,8,128]{2,1,0:T(8,128)S(1)} %get-tuple-element.35, pred[128,1568]{0,1:T(8,128)(4,1)S(1)} %iota_compare_fusion), kind=kLoop, calls=%fused_computation.6 | loop fusion | flops 16054272 | bytes 13062144 | tf_op jit(solution)/shard_map/while/body/eval_jaxpr/reduce_sum | solution.py:38
  25.8 1.5 copy-done.1
  27.4 0.7 reshape.433
  28.1 5.4 %all-to-all-start.2 = ((f32[4,1,512]{2,1,0:T(1,128)}), f32[4,1,512]{2,1,0:T(1,128)S(1)}, u32[]{:S(2)}, u32[]{:S(2)}) async-start(f32[4,1,512]{2,1,0:T(1,128)} %reshape.433), calls=%async_computation.2 | async-start | bytes 16384 | tf_op jit(solution)/shard_map/all_to_all | solution.py:116
  33.7 0.7 reshape.431
  34.4 0.7 copy.130
  35.0 4.1 %all-to-all-done.2 = f32[4,1,512]{2,1,0:T(1,128)S(1)} async-done(((f32[4,1,512]{2,1,0:T(1,128)}), f32[4,1,512]{2,1,0:T(1,128)S(1)}, u32[]{:S(2)}, u32[]{:S(2)}) %all-to-all-start.2) | async-done | bytes 8224 | tf_op jit(solution)/shard_map/all_to_all | solution.py:116
  39.1 3.2 %all-to-all-start = ((f32[4,1,512]{2,1,0:T(1,128)}), f32[4,1,512]{2,1,0:T(1,128)S(1)}, u32[]{:S(2)}, u32[]{:S(2)}) async-start(f32[4,1,512]{2,1,0:T(1,128)} %reshape.431), calls=%async_computation | async-start | bytes 16384 | tf_op jit(solution)/shard_map/all_to_all | solution.py:115
  42.4 6.5 %fusion.5 = f32[2,128,8,128]{3,1,2,0:T(8,128)S(1)} fusion(bf16[1568,2,128,1]{0,2,3,1:T(8,128)(2,1)S(1)} %bitcast.131, f32[2,1568,128,8]{2,1,3,0:T(8,128)} %copy-done.1, f32[2,8,128]{2,1,0:T(8,128)S(1)} %get-tuple-element.35, pred[128,1568]{0,1:T(8,128)(4,1)S(1)} %iota_compare_fusion), kind=kOutput, calls=%fused_computation.9 | convolution fusion | flops 838139904 | bytes 14905344 | tf_op jit(solution)/shard_map/while/body/eval_jaxpr/ekgtp,epkd->etkgd/dot_general | solution.py:39
  48.9 1.4 copy.132
  50.3 5.0 %all-to-all-start.1 = ((f32[128,16,128]{2,1,0:T(8,128)}), f32[128,16,128]{2,1,0:T(8,128)S(1)}, u32[]{:S(2)}, u32[]{:S(2)}) async-start(f32[128,16,128]{2,1,0:T(8,128)} %copy.132), calls=%async_computation.1 | async-start | bytes 2097152 | tf_op jit(solution)/shard_map/all_to_all | solution.py:114
  55.4 0.4 select_reduce_fusion
  55.8 0.2 reduce_window_sum.11
  56.1 0.1 select_reduce_fusion.1
  56.3 12.3 %gather_fusion = bf16[32,128,2,256]{3,2,1,0:T(2,128)(2,1)} fusion(bf16[32,128,2,256]{3,2,1,0:T(2,128)(2,1)} %param.22, s32[1024]{0:T(1024)S(1)} %pad_clamp_fusion.1), kind=kCustom, calls=%fused_computation | custom fusion | bytes 8388736 | tf_op jit(solution)/shard_map/gather | solution.py:144
  68.7 7.4 %all-to-all-done.1 = f32[128,16,128]{2,1,0:T(8,128)S(1)} async-done(((f32[128,16,128]{2,1,0:T(8,128)}), f32[128,16,128]{2,1,0:T(8,128)S(1)}, u32[]{:S(2)}, u32[]{:S(2)}) %all-to-all-start.1) | async-done | bytes 1048608 | tf_op jit(solution)/shard_map/all_to_all | solution.py:114
  76.0 5.0 %all-to-all-start.3 = ((bf16[32,128,2,256]{3,2,1,0:T(2,128)(2,1)}), bf16[32,128,2,256]{3,2,1,0:T(2,128)(2,1)}, u32[]{:S(2)}, u32[]{:S(2)}) async-start(bf16[32,128,2,256]{3,2,1,0:T(2,128)(2,1)} %gather_fusion), calls=%async_computation.3 | async-start | bytes 8388608 | tf_op jit(solution)/shard_map/all_to_all | solution.py:171
  81.2 0.2 fusion.49
  81.4 5.8 %psum.7 = bf16[16,128]{1,0:T(8,128)(2,1)S(1)} all-reduce(f32[16,128]{1,0:T(8,128)S(1)} %fusion.49), channel_id=1, replica_groups=mesh['groups'=2,'seq'=4,'tensor'=4] {'tensor'}, use_global_device_ids=true, to_apply=%region_12.13 | all-reduce | flops 2048 | bytes 12288 | tf_op jit(solution)/shard_map/psum | solution.py:155
  87.2 0.2 select_reduce_fusion.4
  87.4 0.2 fusion.28
  87.8 0.2 select_reduce_fusion.2
  88.1 0.2 convert_reduce_fusion
  88.4 0.5 broadcast.338
  88.9 0.7 reduce.4
  89.7 0.7 reduce.3
  90.6 0.3 multiply_reduce_fusion
  91.0 0.1 divide_convert_fusion
  91.1 0.7 copy.168
  91.8 78.9 %all-to-all-done.3 = bf16[32,128,2,256]{3,2,1,0:T(2,128)(2,1)} async-done(((bf16[32,128,2,256]{3,2,1,0:T(2,128)(2,1)}), bf16[32,128,2,256]{3,2,1,0:T(2,128)(2,1)}, u32[]{:S(2)}, u32[]{:S(2)}) %all-to-all-start.3) | async-done | bytes 4194336 | tf_op jit(solution)/shard_map/all_to_all | solution.py:171
  170.8 5.0 %copy.136 = bf16[32,128,2,256]{3,1,2,0:T(8,128)(2,1)} copy(bf16[32,128,2,256]{3,2,1,0:T(2,128)(2,1)} %all-to-all-done.3) | data formatting | bytes 8388608 | tf_op jit(solution)/shard_map/all_to_all | solution.py:171
  175.8 4.9 %gather_fusion.1 = bf16[32,128,2,256]{3,1,2,0:T(8,128)(2,1)} fusion(bf16[32,128,2,256]{3,1,2,0:T(8,128)(2,1)} %copy.136, s32[1024]{0:T(1024)S(1)} %pad_clamp_fusion), kind=kCustom, calls=%fused_computation.1 | custom fusion | bytes 8388736 | tf_op jit(solution)/shard_map/gather | solution.py:172
  180.7 2.5 %copy.137 = bf16[32,128,2,256]{3,1,0,2:T(8,128)(2,1)S(1)} copy(bf16[32,128,2,256]{3,1,2,0:T(8,128)(2,1)} %gather_fusion.1) | data formatting | bytes 8388608 | tf_op jit(solution)/shard_map/gather | solution.py:172
  183.2 2.3 %fusion.45 = (bf16[4,1024,1,256]{3,1,0,2:T(8,128)(2,1)}, bf16[4,1024,1,256]{3,1,0,2:T(8,128)(2,1)}) fusion(bf16[4,1024,2,256]{3,1,0,2:T(8,128)(2,1)S(1)} %bitcast.124), kind=kLoop, calls=%fused_computation.94 | loop fusion | bytes 8388608 | tf_op jit(solution)/shard_map/slice | solution.py:173
  185.5 3.0 %copy.140 = bf16[4,1024,1,256]{1,3,0,2:T(8,128)(2,1)S(1)} copy(bf16[4,1024,1,256]{3,1,0,2:T(8,128)(2,1)} %get-tuple-element.33) | data formatting | bytes 4194304 | tf_op jit(solution)/shard_map/slice | solution.py:173
  188.4 2.6 %copy.141 = bf16[4,1024,2,128]{3,1,2,0:T(8,128)(2,1)} copy(bf16[4,1024,2,128]{1,3,2,0:T(8,128)(2,1)S(1)} %bitcast.125) | data formatting | bytes 4194304 | tf_op jit(solution)/shard_map/concatenate | solution.py:173
  191.0 3.0 %copy.138 = bf16[4,1024,1,256]{1,3,0,2:T(8,128)(2,1)S(1)} copy(bf16[4,1024,1,256]{3,1,0,2:T(8,128)(2,1)} %get-tuple-element.34) | data formatting | bytes 4194304 | tf_op jit(solution)/shard_map/slice | solution.py:174
  194.0 2.6 %copy.139 = bf16[4,1024,2,128]{3,1,2,0:T(8,128)(2,1)} copy(bf16[4,1024,2,128]{1,3,2,0:T(8,128)(2,1)S(1)} %bitcast.126) | data formatting | bytes 4194304 | tf_op jit(solution)/shard_map/concatenate | solution.py:174
  196.6 2.7 %fusion.46 = (f32[4,2,8,4]{2,3,1,0:T(4,128)S(1)}, bf16[4,2,8,4,1028]{4,2,3,1,0:T(8,128)(2,1)S(1)}) fusion(bf16[4,4,2,128]{3,1,2,0:T(4,128)(2,1)S(1)} %bitcast.140, bf16[4,1024,2,128]{3,1,2,0:T(8,128)(2,1)} %copy.141, pred[4,4,1028]{2,1,0:T(4,128)(4,1)S(1)} %pad_add_fusion, bf16[4,4,2,8,128]{4,3,2,1,0:T(8,128)(2,1)S(1)} %reshape.409), kind=kOutput, calls=%fused_computation.95 | convolution fusion | flops 73161728 | bytes 2714688 | tf_op jit(solution)/shard_map/sub | solution.py:37
  199.4 0.5 fusion.18
  200.0 0.1 div.52
  200.2 0.7 divide_convert_fusion.1
  (71 shorter events, 1.7 us)
Async XLA Ops:
  0.6 86.8 %copy-start = (bf16[128,2048]{1,0:T(8,128)(2,1)S(1)}, bf16[128,2048]{1,0:T(8,128)(2,1)}, u32[]{:S(2)}) copy-start(bf16[128,2048]{1,0:T(8,128)(2,1)} %param.28) | copy-start | bytes 1572868
  22.7 4.6 %copy-start.1 = (f32[2,1568,128,8]{2,1,3,0:T(8,128)}, f32[2,1568,128,8]{2,1,3,0:T(8,128)S(1)}, u32[]{:S(2)}) copy-start(f32[2,1568,128,8]{2,1,3,0:T(8,128)S(1)} %get-tuple-element.36) | copy-start | bytes 38535172
  22.8 10.8 %copy-start.3 = (bf16[1536,256]{1,0:T(8,128)(2,1)S(1)}, bf16[1536,256]{1,0:T(8,128)(2,1)}, u32[]{:S(2)}) copy-start(bf16[1536,256]{1,0:T(8,128)(2,1)} %param.21) | copy-start | bytes 2359300
  22.8 10.8 %copy-start.7 = (bf16[32,256]{1,0:T(8,128)(2,1)S(1)}, bf16[32,256]{1,0:T(8,128)(2,1)}, u32[]{:S(2)}) copy-start(bf16[32,256]{1,0:T(8,128)(2,1)} %param.19) | copy-start | bytes 49156
  28.1 11.0 %all-to-all-start.2 = ((f32[4,1,512]{2,1,0:T(1,128)}), f32[4,1,512]{2,1,0:T(1,128)S(1)}, u32[]{:S(2)}, u32[]{:S(2)}) async-start(f32[4,1,512]{2,1,0:T(1,128)} %reshape.433), calls=%async_computation.2 | async-start | bytes 16384 | tf_op jit(solution)/shard_map/all_to_all | solution.py:116
  39.1 11.1 %all-to-all-start = ((f32[4,1,512]{2,1,0:T(1,128)}), f32[4,1,512]{2,1,0:T(1,128)S(1)}, u32[]{:S(2)}, u32[]{:S(2)}) async-start(f32[4,1,512]{2,1,0:T(1,128)} %reshape.431), calls=%async_computation | async-start | bytes 16384 | tf_op jit(solution)/shard_map/all_to_all | solution.py:115
  48.8 6.5 %copy-start.11 = (s32[16]{0:T(128)S(1)}, s32[16]{0:T(128)}, u32[]{:S(2)}) copy-start(s32[16]{0:T(128)} %param.29) | copy-start | bytes 196
  48.8 6.5 %copy-start.8 = (s32[16,8]{0,1:T(8,128)S(1)}, s32[16,8]{0,1:T(8,128)}, u32[]{:S(2)}) copy-start(s32[16,8]{0,1:T(8,128)} %param.30) | copy-start | bytes 1540
  50.3 25.8 %all-to-all-start.1 = ((f32[128,16,128]{2,1,0:T(8,128)}), f32[128,16,128]{2,1,0:T(8,128)S(1)}, u32[]{:S(2)}, u32[]{:S(2)}) async-start(f32[128,16,128]{2,1,0:T(8,128)} %copy.132), calls=%async_computation.1 | async-start | bytes 2097152 | tf_op jit(solution)/shard_map/all_to_all | solution.py:114
  68.6 12.5 %copy-start.5 = (bf16[4,4,2048]{2,1,0:T(4,128)(2,1)S(1)}, bf16[4,4,2048]{2,1,0:T(4,128)(2,1)}, u32[]{:S(2)}) copy-start(bf16[4,4,2048]{2,1,0:T(4,128)(2,1)} %param.26) | copy-start | bytes 196612
  68.6 12.5 %copy-start.4 = (bf16[2048,128]{1,0:T(8,128)(2,1)S(1)}, bf16[2048,128]{1,0:T(8,128)(2,1)}, u32[]{:S(2)}) copy-start(bf16[2048,128]{1,0:T(8,128)(2,1)} %param.27) | copy-start | bytes 1572868
  68.6 18.5 %copy-start.9 = (s32[16]{0:T(128)S(1)}, s32[16]{0:T(128)}, u32[]{:S(2)}) copy-start(s32[16]{0:T(128)} %param.32) | copy-start | bytes 196
  68.7 18.5 %copy-start.10 = (s32[16]{0:T(128)S(1)}, s32[16]{0:T(128)}, u32[]{:S(2)}) copy-start(s32[16]{0:T(128)} %param.33) | copy-start | bytes 196
  68.7 19.0 %copy-start.6 = (bf16[4,4,2048]{2,1,0:T(4,128)(2,1)S(1)}, bf16[4,4,2048]{2,1,0:T(4,128)(2,1)}, u32[]{:S(2)}) copy-start(bf16[4,4,2048]{2,1,0:T(4,128)(2,1)} %param.23) | copy-start | bytes 196612
  68.7 19.1 %copy-start.14 = (s32[16]{0:T(128)S(1)}, s32[16]{0:T(128)}, u32[]{:S(2)}) copy-start(s32[16]{0:T(128)} %param.31) | copy-start | bytes 196
  76.0 94.7 %all-to-all-start.3 = ((bf16[32,128,2,256]{3,2,1,0:T(2,128)(2,1)}), bf16[32,128,2,256]{3,2,1,0:T(2,128)(2,1)}, u32[]{:S(2)}, u32[]{:S(2)}) async-start(bf16[32,128,2,256]{3,2,1,0:T(2,128)(2,1)} %gather_fusion), calls=%async_computation.3 | async-start | bytes 8388608 | tf_op jit(solution)/shard_map/all_to_all | solution.py:171
  191.0 5.6 %copy-start.12 = (bf16[4,4,256]{2,1,0:T(4,128)(2,1)S(1)}, bf16[4,4,256]{2,1,0:T(4,128)(2,1)}, u32[]{:S(2)}) copy-start(bf16[4,4,256]{2,1,0:T(4,128)(2,1)} %param.24) | copy-start | bytes 24580
  196.6 2.7 %copy-start.2 = (bf16[4,1024,2,128]{3,1,2,0:T(8,128)(2,1)S(1)}, bf16[4,1024,2,128]{3,1,2,0:T(8,128)(2,1)}, u32[]{:S(2)}) copy-start(bf16[4,1024,2,128]{3,1,2,0:T(8,128)(2,1)} %copy.139) | copy-start | bytes 6291460
  196.6 2.7 %copy-start.13 = (bf16[4,4,256]{2,1,0:T(4,128)(2,1)S(1)}, bf16[4,4,256]{2,1,0:T(4,128)(2,1)}, u32[]{:S(2)}) copy-start(bf16[4,4,256]{2,1,0:T(4,128)(2,1)} %param.25) | copy-start | bytes 24580
where the time goes:
time: 202 us; the launch traced here: 201 us
  waiting for transfers between devices  90.4 us (45%)
  local copies, waits for them, and re-layouts  46.6 us (23%)
  blocking collectives  23.3 us (12%)
  starting transfers between devices  18.7 us (9%)
  matrix products  12.1 us (6%)
  other arithmetic  8.73 us (4%)
    all_to_all x1, waiting for transfers between devices, per_device(): lax.all_to_all(outgoing, 'seq', split_axis=0, concat_axis=0, tiled=True)  78.9 us
    all_gather x1, blocking collectives, per_device(): everyone = lax.all_gather(final_block_queries, 'seq', axis=0, tiled=True)  17.6 us
    gather x1, local copies, waits for them, and re-layouts, per_device(): outgoing = paged_cache_pool[send_place]  12.3 us
    gather x2, local copies, waits for them, and re-layouts, per_device(): incoming[arrive].reshape(slots_here, page_count * page_len, 2, -1)  7.38 us
    all_to_all x1, waiting for transfers between devices, per_device(): lax.all_to_all(summed, 'seq', split_axis=0, concat_axis=0, tiled=True)  7.36 us
    dot_general x2, matrix products, partial_softmax(): jnp.einsum('ekgtp,epkd->etkgd', weights.astype(jnp.bfloat16), value_head_...  6.91 us
    psum x1, blocking collectives, per_device(): lax.psum(jnp.dot(hidden_input_rows, adapter_down_maps, preferred_element_...  5.75 us
    all_to_all x1, starting transfers between devices, per_device(): lax.all_to_all(row_total, 'seq', split_axis=0, concat_axis=0, tiled=True)  5.39 us
  transfers between devices with their start and end apart: 4, of which 3 were waited for; matrix products, arithmetic and copies ran while one was open for 14% of the time, Pallas kernels for 0%

commit v1 on v0

--- a/solution.py
+++ b/solution.py
@@ -88,7 +88,22 @@
     span_rows = final_block_queries.shape[0]
     ctx_rows = prompt_cached_keys.shape[0]
     heads_here = final_block_queries.shape[1] // HEAD_SIZE
-    everyone = lax.all_gather(final_block_queries, "seq", axis=0, tiled=True)
+    p_count = lax.axis_size("seq")
+    made = []
+    for t in [*range(p_count)]:
+        made.append((t, (t + 1) % p_count))
+    gallery = []
+    for t in [*range(p_count)]:
+        gallery.append((t, (t - 1) % p_count))
+    z1, local_next = ([final_block_queries], [final_block_queries])
+    for _ in range(p_count // 2):
+        z1.append(lax.ppermute(z1[-1], "seq", made))
+    for _ in [*range((p_count - 1) // 2)]:
+        local_next.append(lax.ppermute(local_next[-1], "seq", gallery))
+    view_out = jnp.concatenate([*z1[::-1], *local_next[1:]], 0)
+    everyone = jnp.roll(
+        view_out, (lax.axis_index("seq") - p_count // 2) * final_block_queries.shape[0], 0
+    )
     span_total = everyone.shape[0]
     block_rows = min(128, span_total)
     paged_key_rows = jnp.concatenate([prompt_cached_keys, final_block_keys], axis=0)

time: 202 us -> 228 us (1.13)
  waiting for transfers between devices: 90.4 us -> 125 us
  blocking collectives: 23.3 us -> 5.75 us
  local copies, waits for them, and re-layouts: 46.6 us -> 52.9 us
  starting transfers between devices: 18.7 us -> 21.6 us
    ppermute x0 -> x3, waiting for transfers between devices: none -> 32.3 us  [the longest x2 24.2 us: per_device(): z1.append(lax.ppermute(z1[-1], 'seq', made))]
    all_gather x1 -> x0, blocking collectives: 17.6 us -> none  [per_device(): everyone = lax.all_gather(final_block_queries, 'seq', axis=0, tiled=True)]
    ppermute x0 -> x3, starting transfers between devices: none -> 5.2 us  [the longest x2 3.11 us: per_device(): z1.append(lax.ppermute(z1[-1], 'seq', made))]
    concatenate x0 -> x1, local copies, waits for them, and re-layouts: none -> 5.11 us  [per_device(): jnp.roll(view_out, (lax.axis_index('seq') - p_count // 2) * final_block_q...]
    unnamed x35 -> x36, local copies, waits for them, and re-layouts: 3.81 us -> 5.05 us
  transfers between devices with their start and end apart: 4 -> 7, of which waited for: 3 -> 6; matrix products, arithmetic and copies ran while one was open for 14% -> 13% of each run, Pallas kernels for 0% -> 0%
where the time goes in v1:
time: 228 us; the launch traced here: 227 us
  waiting for transfers between devices  125 us (55%)
  local copies, waits for them, and re-layouts  52.9 us (23%)
  starting transfers between devices  21.6 us (9%)
  matrix products  12.1 us (5%)
  other arithmetic  8.73 us (4%)
  blocking collectives  5.75 us (3%)
    all_to_all x1, waiting for transfers between devices, per_device(): lax.all_to_all(outgoing, 'seq', split_axis=0, concat_axis=0, tiled=True)  80.4 us
    ppermute x2, waiting for transfers between devices, per_device(): z1.append(lax.ppermute(z1[-1], 'seq', made))  24.2 us
    gather x1, local copies, waits for them, and re-layouts, per_device(): outgoing = paged_cache_pool[send_place]  12.3 us
    all_to_all x1, waiting for transfers between devices, per_device(): lax.all_to_all(summed, 'seq', split_axis=0, concat_axis=0, tiled=True)  8.36 us
    ppermute x1, waiting for transfers between devices, per_device(): local_next.append(lax.ppermute(local_next[-1], 'seq', gallery))  8.11 us
    gather x2, local copies, waits for them, and re-layouts, per_device(): incoming[arrive].reshape(slots_here, page_count * page_len, 2, -1)  7.38 us
    dot_general x2, matrix products, partial_softmax(): jnp.einsum('ekgtp,epkd->etkgd', weights.astype(jnp.bfloat16), value_head_...  6.91 us
    psum x1, blocking collectives, per_device(): lax.psum(jnp.dot(hidden_input_rows, adapter_down_maps, preferred_element_...  5.75 us
  transfers between devices with their start and end apart: 7, of which 6 were waited for; matrix products, arithmetic and copies ran while one was open for 13% of the time, Pallas kernels for 0%

profile of v1, /device:TPU:0, one launch (start us, length us, event | category | flops | bytes accessed | tf_op | source)
XLA Modules:
  0.0 227.2 jit_solution(6373391852047155564)
XLA Ops:
  0.6 1.2 copy.143
  1.9 3.1 %collective-permute-start = (bf16[32,2048]{0,1:T(8,128)(2,1)S(1)}, bf16[32,2048]{0,1:T(8,128)(2,1)}, u32[]{:S(2)}, u32[]{:S(2)}) collective-permute-start(bf16[32,2048]{0,1:T(8,128)(2,1)S(1)} %copy.143), channel_id=1, source_target_pairs={{0,4},{4,8},{8,12},{12,0},{1,5},{5,9},{9,13},{13,1},{2,6},{6,10},{... | collective-permute-start | bytes 393224 | tf_op jit(solution)/shard_map/ppermute | solution.py:100
  5.0 2.1 collective-permute-start.2
  7.1 0.3 iota_compare_fusion
  7.4 12.6 %collective-permute-done = bf16[32,2048]{0,1:T(8,128)(2,1)} collective-permute-done((bf16[32,2048]{0,1:T(8,128)(2,1)S(1)}, bf16[32,2048]{0,1:T(8,128)(2,1)}, u32[]{:S(2)}, u32[]{:S(2)}) %collective-permute-start) | collective-permute-done | bytes 131104 | tf_op jit(solution)/shard_map/ppermute | solution.py:100
  19.9 1.2 pad_maximum_fusion
  21.2 0.7 copy.142
  21.8 8.1 %collective-permute-done.2 = bf16[32,2048]{0,1:T(8,128)(2,1)} collective-permute-done((bf16[32,2048]{0,1:T(8,128)(2,1)S(1)}, bf16[32,2048]{0,1:T(8,128)(2,1)}, u32[]{:S(2)}, u32[]{:S(2)}) %collective-permute-start.2) | collective-permute-done | bytes 131104 | tf_op jit(solution)/shard_map/ppermute | solution.py:102
  29.9 11.6 %collective-permute-done.1 = bf16[32,2048]{0,1:T(8,128)(2,1)} collective-permute-done((bf16[32,2048]{0,1:T(8,128)(2,1)}, bf16[32,2048]{0,1:T(8,128)(2,1)}, u32[]{:S(2)}, u32[]{:S(2)}) %collective-permute-start.1) | collective-permute-done | bytes 131104 | tf_op jit(solution)/shard_map/ppermute | solution.py:100
  41.6 5.1 %concatenate.32 = bf16[256,2048]{0,1:T(8,128)(2,1)S(1)} concatenate(bf16[32,2048]{0,1:T(8,128)(2,1)} %collective-permute-done.1, bf16[32,2048]{0,1:T(8,128)(2,1)} %collective-permute-done, bf16[32,2048]{0,1:T(8,128)(2,1)S(1)} %copy.143, bf16[32,2048]{0,1:T(8,128)(2,1)} %collective-permute-done.2, bf16[32,2048]{0,1:T(8,128)(2,1)} %collective-permute-done.1, ...), dimensions={0} | concatenate | bytes 2097152 | tf_op jit(solution)/shard_map/jit(_roll_dynamic)/concatenate | solution.py:104
  46.7 0.2 constant_dynamic-slice_fusion.1
  46.9 2.0 fusion.1
  49.0 3.0 %fusion.2 = f32[2,8,128]{2,1,0:T(8,128)S(1)} fusion(f32[2,1568,128,8]{2,1,3,0:T(8,128)S(1)} %get-tuple-element.36, f32[2,8,128]{2,1,0:T(8,128)S(1)} %get-tuple-element.35, pred[128,1568]{0,1:T(8,128)(4,1)S(1)} %iota_compare_fusion), kind=kLoop, calls=%fused_computation.6 | loop fusion | flops 16054272 | bytes 13062144 | tf_op jit(solution)/shard_map/while/body/eval_jaxpr/reduce_sum | solution.py:38
  52.0 1.5 copy-done.1
  53.7 0.7 reshape.433
  54.3 3.2 %all-to-all-start.2 = ((f32[4,1,512]{2,1,0:T(1,128)}), f32[4,1,512]{2,1,0:T(1,128)S(1)}, u32[]{:S(2)}, u32[]{:S(2)}) async-start(f32[4,1,512]{2,1,0:T(1,128)} %reshape.433), calls=%async_computation.2 | async-start | bytes 16384 | tf_op jit(solution)/shard_map/all_to_all | solution.py:131
  57.7 0.7 copy.151
  58.5 0.7 reshape.431
  59.1 4.0 %all-to-all-done.2 = f32[4,1,512]{2,1,0:T(1,128)S(1)} async-done(((f32[4,1,512]{2,1,0:T(1,128)}), f32[4,1,512]{2,1,0:T(1,128)S(1)}, u32[]{:S(2)}, u32[]{:S(2)}) %all-to-all-start.2) | async-done | bytes 8224 | tf_op jit(solution)/shard_map/all_to_all | solution.py:131
  63.2 3.2 %all-to-all-start = ((f32[4,1,512]{2,1,0:T(1,128)}), f32[4,1,512]{2,1,0:T(1,128)S(1)}, u32[]{:S(2)}, u32[]{:S(2)}) async-start(f32[4,1,512]{2,1,0:T(1,128)} %reshape.431), calls=%async_computation | async-start | bytes 16384 | tf_op jit(solution)/shard_map/all_to_all | solution.py:130
  66.4 6.5 %fusion.5 = f32[2,128,8,128]{3,1,2,0:T(8,128)S(1)} fusion(bf16[1568,2,128,1]{0,2,3,1:T(8,128)(2,1)S(1)} %bitcast.131, f32[2,1568,128,8]{2,1,3,0:T(8,128)} %copy-done.1, f32[2,8,128]{2,1,0:T(8,128)S(1)} %get-tuple-element.35, pred[128,1568]{0,1:T(8,128)(4,1)S(1)} %iota_compare_fusion), kind=kOutput, calls=%fused_computation.9 | convolution fusion | flops 838139904 | bytes 14905344 | tf_op jit(solution)/shard_map/while/body/eval_jaxpr/ekgtp,epkd->etkgd/dot_general | solution.py:39
  72.9 1.4 copy.153
  74.3 5.0 %all-to-all-start.1 = ((f32[128,16,128]{2,1,0:T(8,128)}), f32[128,16,128]{2,1,0:T(8,128)S(1)}, u32[]{:S(2)}, u32[]{:S(2)}) async-start(f32[128,16,128]{2,1,0:T(8,128)} %copy.153), calls=%async_computation.1 | async-start | bytes 2097152 | tf_op jit(solution)/shard_map/all_to_all | solution.py:129
  79.4 0.4 select_reduce_fusion
  79.9 0.2 reduce_window_sum.11
  80.4 12.3 %gather_fusion = bf16[32,128,2,256]{3,2,1,0:T(2,128)(2,1)} fusion(bf16[32,128,2,256]{3,2,1,0:T(2,128)(2,1)} %param.22, s32[1024]{0:T(1024)S(1)} %pad_clamp_fusion.1), kind=kCustom, calls=%fused_computation | custom fusion | bytes 8388736 | tf_op jit(solution)/shard_map/gather | solution.py:159
  92.7 8.4 %all-to-all-done.1 = f32[128,16,128]{2,1,0:T(8,128)S(1)} async-done(((f32[128,16,128]{2,1,0:T(8,128)}), f32[128,16,128]{2,1,0:T(8,128)S(1)}, u32[]{:S(2)}, u32[]{:S(2)}) %all-to-all-start.1) | async-done | bytes 1048608 | tf_op jit(solution)/shard_map/all_to_all | solution.py:129
  101.1 4.9 %all-to-all-start.3 = ((bf16[32,128,2,256]{3,2,1,0:T(2,128)(2,1)}), bf16[32,128,2,256]{3,2,1,0:T(2,128)(2,1)}, u32[]{:S(2)}, u32[]{:S(2)}) async-start(bf16[32,128,2,256]{3,2,1,0:T(2,128)(2,1)} %gather_fusion), calls=%async_computation.3 | async-start | bytes 8388608 | tf_op jit(solution)/shard_map/all_to_all | solution.py:186
  106.3 5.8 %psum.7 = bf16[16,128]{1,0:T(8,128)(2,1)S(1)} all-reduce(f32[16,128]{1,0:T(8,128)S(1)} %fusion.49), channel_id=1, replica_groups=mesh['groups'=2,'seq'=4,'tensor'=4] {'tensor'}, use_global_device_ids=true, to_apply=%region_12.13 | all-reduce | flops 2048 | bytes 12288 | tf_op jit(solution)/shard_map/psum | solution.py:170
  112.0 0.2 select_reduce_fusion.4
  112.3 0.2 fusion.28
  113.3 0.5 broadcast.339
  113.8 0.7 reduce.4
  114.6 0.7 reduce.3
  115.5 0.3 multiply_reduce_fusion
  116.0 0.7 copy.189
  116.7 80.4 %all-to-all-done.3 = bf16[32,128,2,256]{3,2,1,0:T(2,128)(2,1)} async-done(((bf16[32,128,2,256]{3,2,1,0:T(2,128)(2,1)}), bf16[32,128,2,256]{3,2,1,0:T(2,128)(2,1)}, u32[]{:S(2)}, u32[]{:S(2)}) %all-to-all-start.3) | async-done | bytes 4194336 | tf_op jit(solution)/shard_map/all_to_all | solution.py:186
  197.1 5.0 %copy.157 = bf16[32,128,2,256]{3,1,2,0:T(8,128)(2,1)} copy(bf16[32,128,2,256]{3,2,1,0:T(2,128)(2,1)} %all-to-all-done.3) | data formatting | bytes 8388608 | tf_op jit(solution)/shard_map/all_to_all | solution.py:186
  202.2 4.9 %gather_fusion.1 = bf16[32,128,2,256]{3,1,2,0:T(8,128)(2,1)} fusion(bf16[32,128,2,256]{3,1,2,0:T(8,128)(2,1)} %copy.157, s32[1024]{0:T(1024)S(1)} %pad_clamp_fusion), kind=kCustom, calls=%fused_computation.1 | custom fusion | bytes 8388736 | tf_op jit(solution)/shard_map/gather | solution.py:187
  207.1 2.5 %copy.158 = bf16[32,128,2,256]{3,1,0,2:T(8,128)(2,1)S(1)} copy(bf16[32,128,2,256]{3,1,2,0:T(8,128)(2,1)} %gather_fusion.1) | data formatting | bytes 8388608 | tf_op jit(solution)/shard_map/gather | solution.py:187
  209.5 2.3 fusion.45
  211.8 3.0 %copy.161 = bf16[4,1024,1,256]{1,3,0,2:T(8,128)(2,1)S(1)} copy(bf16[4,1024,1,256]{3,1,0,2:T(8,128)(2,1)} %get-tuple-element.33) | data formatting | bytes 4194304 | tf_op jit(solution)/shard_map/slice | solution.py:188
  214.8 2.6 %copy.162 = bf16[4,1024,2,128]{3,1,2,0:T(8,128)(2,1)} copy(bf16[4,1024,2,128]{1,3,2,0:T(8,128)(2,1)S(1)} %bitcast.125) | data formatting | bytes 4194304 | tf_op jit(solution)/shard_map/concatenate | solution.py:188
  217.4 3.0 %copy.159 = bf16[4,1024,1,256]{1,3,0,2:T(8,128)(2,1)S(1)} copy(bf16[4,1024,1,256]{3,1,0,2:T(8,128)(2,1)} %get-tuple-element.34) | data formatting | bytes 4194304 | tf_op jit(solution)/shard_map/slice | solution.py:189
  220.4 2.6 %copy.160 = bf16[4,1024,2,128]{3,1,2,0:T(8,128)(2,1)} copy(bf16[4,1024,2,128]{1,3,2,0:T(8,128)(2,1)S(1)} %bitcast.126) | data formatting | bytes 4194304 | tf_op jit(solution)/shard_map/concatenate | solution.py:189
  223.0 2.7 %fusion.46 = (f32[4,2,8,4]{2,3,1,0:T(4,128)S(1)}, bf16[4,2,8,4,1028]{4,2,3,1,0:T(8,128)(2,1)S(1)}) fusion(bf16[4,4,2,128]{3,1,2,0:T(4,128)(2,1)S(1)} %bitcast.140, bf16[4,1024,2,128]{3,1,2,0:T(8,128)(2,1)} %copy.162, pred[4,4,1028]{2,1,0:T(4,128)(4,1)S(1)} %pad_add_fusion, bf16[4,4,2,8,128]{4,3,2,1,0:T(8,128)(2,1)S(1)} %reshape.409), kind=kOutput, calls=%fused_computation.96 | convolution fusion | flops 73161728 | bytes 2714688 | tf_op jit(solution)/shard_map/sub | solution.py:37
  225.7 0.5 fusion.18
  226.5 0.7 divide_convert_fusion.1
  (78 shorter events, 2.6 us)
Async XLA Ops:
  0.6 111.7 %copy-start = (bf16[128,2048]{1,0:T(8,128)(2,1)S(1)}, bf16[128,2048]{1,0:T(8,128)(2,1)}, u32[]{:S(2)}) copy-start(bf16[128,2048]{1,0:T(8,128)(2,1)} %param.28) | copy-start | bytes 1572868
  1.9 18.1 %collective-permute-start = (bf16[32,2048]{0,1:T(8,128)(2,1)S(1)}, bf16[32,2048]{0,1:T(8,128)(2,1)}, u32[]{:S(2)}, u32[]{:S(2)}) collective-permute-start(bf16[32,2048]{0,1:T(8,128)(2,1)S(1)} %copy.143), channel_id=1, source_target_pairs={{0,4},{4,8},{8,12},{12,0},{1,5},{5,9},{9,13},{13,1},{2,6},{6,10},{... | collective-permute-start | bytes 393224 | tf_op jit(solution)/shard_map/ppermute | solution.py:100
  5.0 25.0 %collective-permute-start.2 = (bf16[32,2048]{0,1:T(8,128)(2,1)S(1)}, bf16[32,2048]{0,1:T(8,128)(2,1)}, u32[]{:S(2)}, u32[]{:S(2)}) collective-permute-start(bf16[32,2048]{0,1:T(8,128)(2,1)S(1)} %copy.143), channel_id=1, source_target_pairs={{0,12},{4,0},{8,4},{12,8},{1,13},{5,1},{9,5},{13,9},{2,14},{6,2},{... | collective-permute-start | bytes 393224 | tf_op jit(solution)/shard_map/ppermute | solution.py:102
  19.9 21.6 %collective-permute-start.1 = (bf16[32,2048]{0,1:T(8,128)(2,1)}, bf16[32,2048]{0,1:T(8,128)(2,1)}, u32[]{:S(2)}, u32[]{:S(2)}) collective-permute-start(bf16[32,2048]{0,1:T(8,128)(2,1)} %collective-permute-done), channel_id=1, source_target_pairs={{0,4},{4,8},{8,12},{12,0},{1,5},{5,9},{9,13},{13,1},{2,6},{6,10},{... | collective-permute-start | bytes 393224 | tf_op jit(solution)/shard_map/ppermute | solution.py:100
  49.0 4.6 %copy-start.1 = (f32[2,1568,128,8]{2,1,3,0:T(8,128)}, f32[2,1568,128,8]{2,1,3,0:T(8,128)S(1)}, u32[]{:S(2)}) copy-start(f32[2,1568,128,8]{2,1,3,0:T(8,128)S(1)} %get-tuple-element.36) | copy-start | bytes 38535172
  49.0 8.6 %copy-start.3 = (bf16[1536,256]{1,0:T(8,128)(2,1)S(1)}, bf16[1536,256]{1,0:T(8,128)(2,1)}, u32[]{:S(2)}) copy-start(bf16[1536,256]{1,0:T(8,128)(2,1)} %param.21) | copy-start | bytes 2359300
  49.0 8.6 %copy-start.7 = (bf16[32,256]{1,0:T(8,128)(2,1)S(1)}, bf16[32,256]{1,0:T(8,128)(2,1)}, u32[]{:S(2)}) copy-start(bf16[32,256]{1,0:T(8,128)(2,1)} %param.19) | copy-start | bytes 49156
  54.3 8.8 %all-to-all-start.2 = ((f32[4,1,512]{2,1,0:T(1,128)}), f32[4,1,512]{2,1,0:T(1,128)S(1)}, u32[]{:S(2)}, u32[]{:S(2)}) async-start(f32[4,1,512]{2,1,0:T(1,128)} %reshape.433), calls=%async_computation.2 | async-start | bytes 16384 | tf_op jit(solution)/shard_map/all_to_all | solution.py:131
  63.2 11.1 %all-to-all-start = ((f32[4,1,512]{2,1,0:T(1,128)}), f32[4,1,512]{2,1,0:T(1,128)S(1)}, u32[]{:S(2)}, u32[]{:S(2)}) async-start(f32[4,1,512]{2,1,0:T(1,128)} %reshape.431), calls=%async_computation | async-start | bytes 16384 | tf_op jit(solution)/shard_map/all_to_all | solution.py:130
  72.9 6.5 %copy-start.11 = (s32[16]{0:T(128)S(1)}, s32[16]{0:T(128)}, u32[]{:S(2)}) copy-start(s32[16]{0:T(128)} %param.29) | copy-start | bytes 196
  72.9 6.5 %copy-start.8 = (s32[16,8]{0,1:T(8,128)S(1)}, s32[16,8]{0,1:T(8,128)}, u32[]{:S(2)}) copy-start(s32[16,8]{0,1:T(8,128)} %param.30) | copy-start | bytes 1540
  74.3 26.8 %all-to-all-start.1 = ((f32[128,16,128]{2,1,0:T(8,128)}), f32[128,16,128]{2,1,0:T(8,128)S(1)}, u32[]{:S(2)}, u32[]{:S(2)}) async-start(f32[128,16,128]{2,1,0:T(8,128)} %copy.153), calls=%async_computation.1 | async-start | bytes 2097152 | tf_op jit(solution)/shard_map/all_to_all | solution.py:129
  92.7 13.3 %copy-start.5 = (bf16[4,4,2048]{2,1,0:T(4,128)(2,1)S(1)}, bf16[4,4,2048]{2,1,0:T(4,128)(2,1)}, u32[]{:S(2)}) copy-start(bf16[4,4,2048]{2,1,0:T(4,128)(2,1)} %param.26) | copy-start | bytes 196612
  92.7 13.4 %copy-start.4 = (bf16[2048,128]{1,0:T(8,128)(2,1)S(1)}, bf16[2048,128]{1,0:T(8,128)(2,1)}, u32[]{:S(2)}) copy-start(bf16[2048,128]{1,0:T(8,128)(2,1)} %param.27) | copy-start | bytes 1572868
  92.7 19.3 %copy-start.9 = (s32[16]{0:T(128)S(1)}, s32[16]{0:T(128)}, u32[]{:S(2)}) copy-start(s32[16]{0:T(128)} %param.32) | copy-start | bytes 196
  92.7 19.3 %copy-start.10 = (s32[16]{0:T(128)S(1)}, s32[16]{0:T(128)}, u32[]{:S(2)}) copy-start(s32[16]{0:T(128)} %param.33) | copy-start | bytes 196
  92.7 19.8 %copy-start.6 = (bf16[4,4,2048]{2,1,0:T(4,128)(2,1)S(1)}, bf16[4,4,2048]{2,1,0:T(4,128)(2,1)}, u32[]{:S(2)}) copy-start(bf16[4,4,2048]{2,1,0:T(4,128)(2,1)} %param.23) | copy-start | bytes 196612
  92.7 19.9 %copy-start.14 = (s32[16]{0:T(128)S(1)}, s32[16]{0:T(128)}, u32[]{:S(2)}) copy-start(s32[16]{0:T(128)} %param.31) | copy-start | bytes 196
  101.1 96.0 %all-to-all-start.3 = ((bf16[32,128,2,256]{3,2,1,0:T(2,128)(2,1)}), bf16[32,128,2,256]{3,2,1,0:T(2,128)(2,1)}, u32[]{:S(2)}, u32[]{:S(2)}) async-start(bf16[32,128,2,256]{3,2,1,0:T(2,128)(2,1)} %gather_fusion), calls=%async_computation.3 | async-start | bytes 8388608 | tf_op jit(solution)/shard_map/all_to_all | solution.py:186
  217.4 5.6 %copy-start.12 = (bf16[4,4,256]{2,1,0:T(4,128)(2,1)S(1)}, bf16[4,4,256]{2,1,0:T(4,128)(2,1)}, u32[]{:S(2)}) copy-start(bf16[4,4,256]{2,1,0:T(4,128)(2,1)} %param.24) | copy-start | bytes 24580
  223.0 2.7 %copy-start.2 = (bf16[4,1024,2,128]{3,1,2,0:T(8,128)(2,1)S(1)}, bf16[4,1024,2,128]{3,1,2,0:T(8,128)(2,1)}, u32[]{:S(2)}) copy-start(bf16[4,1024,2,128]{3,1,2,0:T(8,128)(2,1)} %copy.160) | copy-start | bytes 6291460
  223.0 2.7 %copy-start.13 = (bf16[4,4,256]{2,1,0:T(4,128)(2,1)S(1)}, bf16[4,4,256]{2,1,0:T(4,128)(2,1)}, u32[]{:S(2)}) copy-start(bf16[4,4,256]{2,1,0:T(4,128)(2,1)} %param.25) | copy-start | bytes 24580
